TPU v7x, 128 devices: a whole 4x4x4 slice. The times are simulated.
128 devices in a mesh: dp: 1, tp: 2 (over core), cp: 64 (over z, y, x).
Axes of the slice: x: 4, y: 4, z: 4, core: 2. Of those that a mesh axis runs over, the one named last changes fastest.
Arguments:
- x: bfloat16 [4096, 2048], P(('dp', 'cp', 'tp'))
- pos: int32 [4096], P(('dp', 'cp', 'tp'))
- g1: bfloat16 [2048], replicated
- g2: bfloat16 [2048], replicated
- wq: bfloat16 [2048, 2048], P(None, 'tp')
- wk: bfloat16 [2048, 256], P(None, 'tp')
- wv: bfloat16 [2048, 256], P(None, 'tp')
- wo: bfloat16 [2048, 2048], P('tp')
- w1: bfloat16 [2048, 11008], P(None, 'tp')
- w3: bfloat16 [2048, 11008], P(None, 'tp')
- w2: bfloat16 [11008, 2048], P('tp')
Outputs:
- output: bfloat16 [4096, 2048], P(('dp', 'cp', 'tp'))
All inputs are finite; a program needn't handle non-finite values.
Results may differ from a plain program's by a relative error of at most 0.0111242.
Values are sent between devices in bfloat16 or wider.
A program may use at most 1 GiB of HBM per device.

v0:
```python
import math
import jax
import jax.numpy as jnp
from jax import lax
from jax.sharding import PartitionSpec as P, NamedSharding

DH = 128
EPS = 1e-5
THETA = 500000.0


def rms_norm(v, g):
    vf = v.astype(jnp.float32)
    inv = lax.rsqrt(jnp.mean(vf * vf, axis=-1, keepdims=True) + EPS)
    return (vf * inv * g.astype(jnp.float32)).astype(jnp.bfloat16)


def rope(y, p):
    half = DH // 2
    freq = 1.0 / (THETA ** (jnp.arange(0, DH, 2, dtype=jnp.float32) / DH))
    ang = p.astype(jnp.float32)[..., None] * freq
    c = jnp.cos(ang)[..., None, :]
    s = jnp.sin(ang)[..., None, :]
    y1 = y[..., :half]
    y2 = y[..., half:]
    return jnp.concatenate([y1 * c - y2 * s, y2 * c + y1 * s], axis=-1)


def attend(q, k, v, qpos, kpos):
    nq, hl, dh = q.shape
    hk = k.shape[1]
    grp = hl // hk
    qb = nq
    while qb % 2 == 0 and qb * hl > 1024:
        qb = qb // 2
    qr = q.reshape(nq // qb, qb, hk, grp, dh)
    pr = qpos.reshape(nq // qb, qb)
    scale = 1.0 / math.sqrt(dh)

    def blk(qp):
        qq, pp = qp
        s = jnp.einsum('qkgd,skd->kgqs', qq, k, preferred_element_type=jnp.float32) * scale
        s = jnp.where(kpos[None, None, None, :] <= pp[None, None, :, None], s, -1e30)
        e = jnp.exp(s - jnp.max(s, axis=-1, keepdims=True))
        w = (e / jnp.sum(e, axis=-1, keepdims=True)).astype(jnp.bfloat16)
        o = jnp.einsum('kgqs,skd->qkgd', w, v, preferred_element_type=jnp.float32)
        return o.astype(jnp.bfloat16)

    return lax.map(blk, (qr, pr)).reshape(nq, hl * dh)


def solution(mesh):
    tok = P(('dp', 'cp', 'tp'), None)
    col = P(None, 'tp')
    row = P('tp', None)

    def local(x, pos, g1, g2, wq, wk, wv, wo, w1, w3, w2):
        a = lax.all_gather(rms_norm(x, g1), 'tp', axis=0, tiled=True)
        pg = lax.all_gather(pos, 'tp', axis=0, tiled=True)
        nr = a.shape[0]
        q = rope(jnp.dot(a, wq, preferred_element_type=jnp.float32).reshape(nr, -1, DH), pg).astype(jnp.bfloat16)
        k = rope(jnp.dot(a, wk, preferred_element_type=jnp.float32).reshape(nr, -1, DH), pg).astype(jnp.bfloat16)
        v = jnp.dot(a, wv, preferred_element_type=jnp.float32).astype(jnp.bfloat16).reshape(nr, -1, DH)
        ka = lax.all_gather(k, 'cp', axis=0, tiled=True)
        va = lax.all_gather(v, 'cp', axis=0, tiled=True)
        pa = lax.all_gather(pg, 'cp', axis=0, tiled=True)
        o = attend(q, ka, va, pg, pa)
        y = lax.psum_scatter(jnp.dot(o, wo, preferred_element_type=jnp.float32), 'tp', scatter_dimension=0, tiled=True)
        h1 = (x.astype(jnp.float32) + y).astype(jnp.bfloat16)
        b = lax.all_gather(rms_norm(h1, g2), 'tp', axis=0, tiled=True)
        hid = (jax.nn.silu(jnp.dot(b, w1, preferred_element_type=jnp.float32)) * jnp.dot(b, w3, preferred_element_type=jnp.float32)).astype(jnp.bfloat16)
        z = lax.psum_scatter(jnp.dot(hid, w2, preferred_element_type=jnp.float32), 'tp', scatter_dimension=0, tiled=True)
        return (h1.astype(jnp.float32) + z).astype(jnp.bfloat16)

    return jax.shard_map(local, mesh=mesh, in_specs=(tok, P(('dp', 'cp', 'tp')), P(None), P(None), col, col, col, row, col, col, row), out_specs=tok, check_vma=False)
```

profile of v0, /device:TPU:1, one launch (start us, length us, event | category | flops | bytes accessed | tf_op | source)
XLA Modules:
  0.0 446.3 jit_solution(4478209610893112184)
XLA Ops:
  6.6 1.3 dynamic-slice.1
  8.5 0.9 dynamic-update-slice
  9.4 2.8 all-reduce
  12.2 0.7 convert_element_type.63
  12.9 1.0 fusion.18
  13.9 1.0 fusion.20
  15.0 2.0 all_gather.18
  17.4 0.7 pad_maximum_fusion
  18.1 1.9 convolution_convert_fusion
  20.3 3.0 convolution_bitcast_fusion
  23.5 0.6 dynamic-slice.2
  25.1 295.0 %all-reduce.1 = s32[4096]{0:T(1024)S(1)} all-reduce(s32[4096]{0:T(1024)S(1)} %dynamic-update-slice.1), channel_id=1, replica_groups=mesh['dp'=1,'tp'=2,'cp'=64] {'cp'}, use_global_device_ids=true, to_apply=%add.1 | all-reduce | flops 4096 | bytes 32768
  320.4 2.9 fusion.44
  323.3 3.2 copy-done.2
  326.5 1.3 fusion
  327.8 5.2 %fusion.12 = bf16[64,1,8,128]{3,0,2,1:T(8,128)(2,1)S(1)} fusion(f32[8,64]{1,0:T(8,128)S(1)} %fusion, f32[1,8,64,4096]{3,2,1,0:T(8,128)} %copy-done.2, f32[8,64]{1,0:T(8,128)S(1)} %get-tuple-element.36, bf16[4096,128]{1,0:T(8,128)(2,1)} %all-gather.6.cloned.1.call-done), kind=kOutput, calls=%fused_computation.15 | convolution fusion | flops 543227904 | bytes 9572352 | tf_op jit(solution)/shard_map/while/body/eval_jaxpr/kgqs,skd->qkgd/dot_general | solution.py:46
  333.1 1.6 fusion.26
  334.8 59.4 %reduce-scatter.3.cloned.1.call-done = f32[32,2048]{1,0:T(8,128)} async-done(((f32[64,2048]{1,0:T(8,128)}), f32[32,2048]{1,0:T(8,128)}) %reduce-scatter.3.cloned.1.call-update) | async-done | bytes 262160 | tf_op jit(solution)/shard_map/reduce_scatter | solution.py:68
  394.3 1.1 fusion.22
  395.5 2.2 all_gather.23
  397.7 9.5 %fusion.45 = f32[64,5504]{1,0:T(8,128)S(1)} fusion(bf16[64,2048]{1,0:T(8,128)(2,1)S(1)} %all_gather.23, bf16[2048,5504]{1,0:T(8,128)(2,1)} %param.19), kind=kOutput, calls=%fused_computation.64 | convolution fusion | flops 1442840576 | bytes 24215552 | tf_op jit(solution)/shard_map/dot_general | solution.py:71
  407.2 18.9 %fusion.4 = f32[64,2048]{1,0:T(8,128)} fusion(bf16[5504,2048]{1,0:T(8,128)(2,1)} %param.21, bf16[64,2048]{1,0:T(8,128)(2,1)S(1)} %all_gather.23, bf16[2048,5504]{1,0:T(8,128)(2,1)} %param.20, f32[64,5504]{1,0:T(8,128)S(1)} %fusion.45), kind=kOutput, calls=%fused_computation.8 | convolution fusion | flops 2887794688 | bytes 47284224 | tf_op jit(solution)/shard_map/dot_general | solution.py:72
  426.1 12.1 %reduce-scatter.5.cloned.1.call-done = f32[32,2048]{1,0:T(8,128)} async-done(((f32[64,2048]{1,0:T(8,128)}), f32[32,2048]{1,0:T(8,128)}) %reduce-scatter.5.cloned.1.call-update) | async-done | bytes 262160 | tf_op jit(solution)/shard_map/reduce_scatter | solution.py:72
  438.1 1.6 fusion.25
  (40 shorter events, 1.9 us)
Async XLA Ops:
  6.5 10.4 %copy-start = (bf16[2048,128]{1,0:T(8,128)(2,1)S(1)}, bf16[2048,128]{1,0:T(8,128)(2,1)}, u32[]{:S(2)}) copy-start(bf16[2048,128]{1,0:T(8,128)(2,1)} %param.16) | copy-start | bytes 1572868
  6.5 17.0 %copy-start.6 = (u32[128]{0:T(128)S(1)}, u32[128]{0:T(128)}, u32[]{:S(2)}) copy-start(u32[128]{0:T(128)} %constant.51) | copy-start | bytes 1540
  6.5 313.8 %all-gather.4.cloned.1.call-start = ((), (), s32[]{:S(2)}) async-start(), calls=%async_computation.2 | async-start | bytes 1064960 | tf_op jit(solution)/shard_map/all_gather | solution.py:64
  18.1 309.7 %all-gather.6.cloned.1.call-start = ((), (), s32[]{:S(2)}) async-start(), calls=%async_computation.5 | async-start | bytes 1064960 | tf_op jit(solution)/shard_map/all_gather | solution.py:65
  20.0 374.2 %reduce-scatter.3.cloned.1.call-start = ((), (), s32[]{:S(2)}) async-start(), calls=%async_computation.3 | async-start | bytes 786432 | tf_op jit(solution)/shard_map/reduce_scatter | solution.py:68
  323.3 3.2 copy-start.2
  327.8 7.0 %copy-start.5 = (bf16[2048]{0:T(1024)(128)(2,1)S(1)}, bf16[2048]{0:T(1024)(128)(2,1)}, u32[]{:S(2)}) copy-start(bf16[2048]{0:T(1024)(128)(2,1)} %param.14) | copy-start | bytes 12292
  327.8 66.5 %copy-start.4 = (bf16[32,2048]{1,0:T(8,128)(2,1)S(1)}, bf16[32,2048]{1,0:T(8,128)(2,1)}, u32[]{:S(2)}) copy-start(bf16[32,2048]{1,0:T(8,128)(2,1)} %param.11) | copy-start | bytes 393220
  327.8 5.3 %copy-start.3 = (bf16[1024,2048]{1,0:T(8,128)(2,1)S(1)}, bf16[1024,2048]{1,0:T(8,128)(2,1)}, u32[]{:S(2)}) copy-start(bf16[1024,2048]{1,0:T(8,128)(2,1)} %param.18) | copy-start | bytes 12582916
  334.7 103.4 %reduce-scatter.5.cloned.1.call-start = ((), (), s32[]{:S(2)}) async-start(), calls=%async_computation.4 | async-start | bytes 786432 | tf_op jit(solution)/shard_map/reduce_scatter | solution.py:72
  407.2 32.6 %copy-start.1 = (bf16[2048,128]{1,0:T(8,128)(2,1)S(1)}, bf16[2048,128]{1,0:T(8,128)(2,1)}, u32[]{:S(2)}) copy-start(bf16[2048,128]{1,0:T(8,128)(2,1)} %param.16) | copy-start | bytes 1572868
Sparse Core Ops, SparseCore 0:
  18.2 64.4 all-gather.3
  85.6 61.4 all-gather.5
  334.9 59.3 reduce-scatter.2
  426.2 11.9 reduce-scatter.4
where the time goes:
time: 447 us; the launch traced here: 446 us
  blocking collectives  302 us (68%)
  waiting for transfers between devices  71.6 us (16%)
  matrix products  43.2 us (10%)
  between operations  14.6 us (3%)
  other arithmetic  8.25 us (2%)
  local copies, waits for them, and re-layouts  6.56 us (1%)
    unnamed x2, blocking collectives  298 us
    reduce_scatter x1, waiting for transfers between devices, local(): lax.psum_scatter(jnp.dot(o, wo, preferred_element_type=jnp.float32), 'tp'...  59.4 us
    dot_general x1, matrix products, local(): jnp.dot(hid, w2, preferred_element_type=jnp.float32)  18.9 us
    reduce_scatter x1, waiting for transfers between devices, local(): lax.psum_scatter(jnp.dot(hid, w2, preferred_element_type=jnp.float32), 't...  12.1 us
    dot_general x1, matrix products, local(): jnp.dot(b, w1, preferred_element_type=jnp.float32)  9.5 us
  transfers between devices with their start and end apart: 4, of which 2 were waited for; matrix products, arithmetic and copies ran while one was open for 2% of the time, Pallas kernels for 0%

commit v1 on v0

--- a/solution.py
+++ b/solution.py
@@ -49,6 +49,14 @@
     return lax.map(blk, (qr, pr)).reshape(nq, hl * dh)
 
 
+def order(c, nr, ncp):
+    i = jnp.arange(nr)
+    piece = nr // 4
+    dev = 2 * c + i // (2 * piece)
+    off = i % (2 * piece)
+    return jnp.where(off < piece, dev * piece + off, (4 * ncp - 1 - dev) * piece + off - piece).astype(jnp.int32)
+
+
 def solution(mesh):
     tok = P(('dp', 'cp', 'tp'), None)
     col = P(None, 'tp')
@@ -63,8 +71,10 @@
         v = jnp.dot(a, wv, preferred_element_type=jnp.float32).astype(jnp.bfloat16).reshape(nr, -1, DH)
         ka = lax.all_gather(k, 'cp', axis=0, tiled=True)
         va = lax.all_gather(v, 'cp', axis=0, tiled=True)
-        pa = lax.all_gather(pg, 'cp', axis=0, tiled=True)
-        o = attend(q, ka, va, pg, pa)
+        ncp = lax.axis_size('cp')
+        oq = order(lax.axis_index('cp'), nr, ncp)
+        ok = jnp.concatenate([order(c, nr, ncp) for c in range(ncp)])
+        o = attend(q, ka, va, oq, ok)
         y = lax.psum_scatter(jnp.dot(o, wo, preferred_element_type=jnp.float32), 'tp', scatter_dimension=0, tiled=True)
         h1 = (x.astype(jnp.float32) + y).astype(jnp.bfloat16)
         b = lax.all_gather(rms_norm(h1, g2), 'tp', axis=0, tiled=True)

time: 447 us -> 217 us (0.49)
  blocking collectives: 302 us -> 7 us
  waiting for transfers between devices: 71.6 us -> 138 us
    unnamed x2 -> x1, blocking collectives: 298 us -> 2.83 us
    all_gather x1, waiting for transfers between devices: 0.02 us -> 58.1 us  [local(): ka = lax.all_gather(k, 'cp', axis=0, tiled=True)]
    all_gather x1, waiting for transfers between devices: 0.01 us -> 56.8 us  [local(): va = lax.all_gather(v, 'cp', axis=0, tiled=True)]
    reduce_scatter x1, waiting for transfers between devices: 59.4 us -> 10.5 us  [local(): lax.psum_scatter(jnp.dot(o, wo, preferred_element_type=jnp.float32), 'tp'...]
  transfers between devices with their start and end apart: 4 -> 4, of which waited for: 2 -> 4; matrix products, arithmetic and copies ran while one was open for 2% -> 5% of each run, Pallas kernels for 0% -> 0%
where the time goes in v1:
time: 217 us; the launch traced here: 216 us
  waiting for transfers between devices  138 us (64%)
  matrix products  43.2 us (20%)
  between operations  14.1 us (6%)
  other arithmetic  8.57 us (4%)
  blocking collectives  7 us (3%)
  local copies, waits for them, and re-layouts  5.82 us (3%)
    all_gather x1, waiting for transfers between devices, local(): ka = lax.all_gather(k, 'cp', axis=0, tiled=True)  58.1 us
    all_gather x1, waiting for transfers between devices, local(): va = lax.all_gather(v, 'cp', axis=0, tiled=True)  56.8 us
    dot_general x1, matrix products, local(): jnp.dot(hid, w2, preferred_element_type=jnp.float32)  18.9 us
    reduce_scatter x1, waiting for transfers between devices, local(): lax.psum_scatter(jnp.dot(hid, w2, preferred_element_type=jnp.float32), 't...  12.1 us
    reduce_scatter x1, waiting for transfers between devices, local(): lax.psum_scatter(jnp.dot(o, wo, preferred_element_type=jnp.float32), 'tp'...  10.5 us
    dot_general x1, matrix products, local(): jnp.dot(b, w1, preferred_element_type=jnp.float32)  9.5 us
    unnamed x15, local copies, waits for them, and re-layouts  5.49 us
    dot_general x1, matrix products, blk(): o = jnp.einsum('kgqs,skd->qkgd', w, v, preferred_element_type=jnp.float32)  5.16 us
  transfers between devices with their start and end apart: 4, of which 4 were waited for; matrix products, arithmetic and copies ran while one was open for 5% of the time, Pallas kernels for 0%

profile of v1, /device:TPU:1, one launch (start us, length us, event | category | flops | bytes accessed | tf_op | source)
XLA Modules:
  0.0 216.4 jit_solution(9144843867075393432)
XLA Ops:
  6.6 1.3 dynamic-slice.1
  8.5 0.9 dynamic-update-slice
  9.4 2.8 %all-reduce = s32[64]{0:T(128)S(1)} all-reduce(s32[64]{0:T(128)S(1)} %dynamic-update-slice), channel_id=1, replica_groups=mesh['dp'=1,'tp'=2,'cp'=64] {'tp'}, use_global_device_ids=true, to_apply=%add | all-reduce | flops 64 | bytes 512
  12.2 0.7 convert_element_type.63
  12.9 1.0 fusion.18
  13.9 1.0 fusion.20
  15.0 2.0 all_gather.15
  17.4 0.7 pad_maximum_fusion
  18.1 1.9 convolution_convert_fusion
  20.7 3.0 %convolution_bitcast_fusion = f32[8,8,8,128]{3,1,2,0:T(8,128)S(1)} fusion(bf16[64,2048]{1,0:T(8,128)(2,1)S(1)} %all_gather.15, bf16[2048,1024]{1,0:T(8,128)(2,1)} %param.15), kind=kOutput, calls=%fused_computation.13 | convolution fusion | flops 268435456 | bytes 4718592 | tf_op jit(solution)/shard_map/dot_general | solution.py:69
  24.4 58.1 %all-gather.4.cloned.1.call-done = bf16[4096,1,128]{2,0,1:T(8,128)(2,1)} async-done(((bf16[64,1,128]{2,0,1:T(8,128)(2,1)}), bf16[4096,1,128]{2,0,1:T(8,128)(2,1)}) %all-gather.4.cloned.1.call-update) | async-done | bytes 1048592 | tf_op jit(solution)/shard_map/all_gather | solution.py:72
  82.5 2.9 %fusion.44 = (f32[8,64]{1,0:T(8,128)S(1)}, f32[1,8,64,4096]{3,2,1,0:T(8,128)S(1)}) fusion(bf16[64,8,64]{2,0,1:T(8,128)(2,1)S(1)} %get-tuple-element.20, bf16[64,8,64]{2,0,1:T(8,128)(2,1)S(1)} %get-tuple-element.19, bf16[4096,1,128]{2,0,1:T(8,128)(2,1)} %all-gather.4.cloned.1.call-done, pred[64,4096]{1,0:T(8,128)(4,1)S(1)} %broadcast_compare_fusion), kind=kOutput, calls=%fused_computation.134 | convolution fusion | flops 543424000 | bytes 9832448 | tf_op jit(solution)/shard_map/while/body/eval_jaxpr/qkgd,skd->kgqs/dot_general | solution.py:42
  85.5 3.3 %copy-done.2 = f32[1,8,64,4096]{3,2,1,0:T(8,128)} copy-done((f32[1,8,64,4096]{3,2,1,0:T(8,128)}, f32[1,8,64,4096]{3,2,1,0:T(8,128)S(1)}, u32[]{:S(2)}) %copy-start.2) | copy-done | bytes 8388632
  88.7 1.3 fusion
  90.0 56.8 %all-gather.6.cloned.1.call-done = bf16[4096,128]{1,0:T(8,128)(2,1)} async-done(((bf16[64,128]{1,0:T(8,128)(2,1)}), bf16[4096,128]{1,0:T(8,128)(2,1)}) %all-gather.6.cloned.1.call-update) | async-done | bytes 1048592 | tf_op jit(solution)/shard_map/all_gather | solution.py:73
  146.8 5.2 %fusion.12 = bf16[64,1,8,128]{3,0,2,1:T(8,128)(2,1)S(1)} fusion(f32[8,64]{1,0:T(8,128)S(1)} %fusion, f32[1,8,64,4096]{3,2,1,0:T(8,128)} %copy-done.2, f32[8,64]{1,0:T(8,128)S(1)} %get-tuple-element.36, bf16[4096,128]{1,0:T(8,128)(2,1)} %all-gather.6.cloned.1.call-done), kind=kOutput, calls=%fused_computation.15 | convolution fusion | flops 543227904 | bytes 9572352 | tf_op jit(solution)/shard_map/while/body/eval_jaxpr/kgqs,skd->qkgd/dot_general | solution.py:46
  152.1 1.6 fusion.26
  153.8 10.5 %reduce-scatter.3.cloned.1.call-done = f32[32,2048]{1,0:T(8,128)} async-done(((f32[64,2048]{1,0:T(8,128)}), f32[32,2048]{1,0:T(8,128)}) %reduce-scatter.3.cloned.1.call-update) | async-done | bytes 262160 | tf_op jit(solution)/shard_map/reduce_scatter | solution.py:78
  164.3 1.1 fusion.22
  165.5 2.2 %all_gather.19 = bf16[64,2048]{1,0:T(8,128)(2,1)S(1)} all-gather(bf16[32,2048]{1,0:T(8,128)(2,1)S(1)} %fusion.24), channel_id=1, replica_groups=mesh['dp'=1,'tp'=2,'cp'=64] {'tp'}, dimensions={0}, use_global_device_ids=true | all-gather | bytes 393216 | tf_op jit(solution)/shard_map/all_gather | solution.py:80
  167.7 9.5 %fusion.45 = f32[64,5504]{1,0:T(8,128)S(1)} fusion(bf16[64,2048]{1,0:T(8,128)(2,1)S(1)} %all_gather.19, bf16[2048,5504]{1,0:T(8,128)(2,1)} %param.19), kind=kOutput, calls=%fused_computation.135 | convolution fusion | flops 1442840576 | bytes 24215552 | tf_op jit(solution)/shard_map/dot_general | solution.py:81
  177.2 18.9 %fusion.4 = f32[64,2048]{1,0:T(8,128)} fusion(bf16[5504,2048]{1,0:T(8,128)(2,1)} %param.21, bf16[64,2048]{1,0:T(8,128)(2,1)S(1)} %all_gather.19, bf16[2048,5504]{1,0:T(8,128)(2,1)} %param.20, f32[64,5504]{1,0:T(8,128)S(1)} %fusion.45), kind=kOutput, calls=%fused_computation.8 | convolution fusion | flops 2887794688 | bytes 47284224 | tf_op jit(solution)/shard_map/dot_general | solution.py:82
  196.1 12.1 %reduce-scatter.5.cloned.1.call-done = f32[32,2048]{1,0:T(8,128)} async-done(((f32[64,2048]{1,0:T(8,128)}), f32[32,2048]{1,0:T(8,128)}) %reduce-scatter.5.cloned.1.call-update) | async-done | bytes 262160 | tf_op jit(solution)/shard_map/reduce_scatter | solution.py:82
  208.2 1.6 fusion.25
  (68 shorter events, 2.0 us)
Async XLA Ops:
  6.5 10.4 %copy-start = (bf16[2048,128]{1,0:T(8,128)(2,1)S(1)}, bf16[2048,128]{1,0:T(8,128)(2,1)}, u32[]{:S(2)}) copy-start(bf16[2048,128]{1,0:T(8,128)(2,1)} %param.16) | copy-start | bytes 1572868
  6.5 76.0 %all-gather.4.cloned.1.call-start = ((), (), s32[]{:S(2)}) async-start(), calls=%async_computation.2 | async-start | bytes 1064960 | tf_op jit(solution)/shard_map/all_gather | solution.py:72
  18.1 128.7 %all-gather.6.cloned.1.call-start = ((), (), s32[]{:S(2)}) async-start(), calls=%async_computation.5 | async-start | bytes 1064960 | tf_op jit(solution)/shard_map/all_gather | solution.py:73
  20.0 144.3 %reduce-scatter.3.cloned.1.call-start = ((), (), s32[]{:S(2)}) async-start(), calls=%async_computation.3 | async-start | bytes 786432 | tf_op jit(solution)/shard_map/reduce_scatter | solution.py:78
  85.5 3.3 %copy-start.2 = (f32[1,8,64,4096]{3,2,1,0:T(8,128)}, f32[1,8,64,4096]{3,2,1,0:T(8,128)S(1)}, u32[]{:S(2)}) copy-start(f32[1,8,64,4096]{3,2,1,0:T(8,128)S(1)} %get-tuple-element.37) | copy-start | bytes 25165828
  90.0 63.8 %copy-start.5 = (bf16[2048]{0:T(1024)(128)(2,1)S(1)}, bf16[2048]{0:T(1024)(128)(2,1)}, u32[]{:S(2)}) copy-start(bf16[2048]{0:T(1024)(128)(2,1)} %param.14) | copy-start | bytes 12292
  90.0 74.3 %copy-start.4 = (bf16[32,2048]{1,0:T(8,128)(2,1)S(1)}, bf16[32,2048]{1,0:T(8,128)(2,1)}, u32[]{:S(2)}) copy-start(bf16[32,2048]{1,0:T(8,128)(2,1)} %param.11) | copy-start | bytes 393220
  146.8 5.3 %copy-start.3 = (bf16[1024,2048]{1,0:T(8,128)(2,1)S(1)}, bf16[1024,2048]{1,0:T(8,128)(2,1)}, u32[]{:S(2)}) copy-start(bf16[1024,2048]{1,0:T(8,128)(2,1)} %param.18) | copy-start | bytes 12582916
  153.8 54.5 %reduce-scatter.5.cloned.1.call-start = ((), (), s32[]{:S(2)}) async-start(), calls=%async_computation.4 | async-start | bytes 786432 | tf_op jit(solution)/shard_map/reduce_scatter | solution.py:82
  177.2 32.6 %copy-start.1 = (bf16[2048,128]{1,0:T(8,128)(2,1)S(1)}, bf16[2048,128]{1,0:T(8,128)(2,1)}, u32[]{:S(2)}) copy-start(bf16[2048,128]{1,0:T(8,128)(2,1)} %param.16) | copy-start | bytes 1572868
Sparse Core Ops, SparseCore 0:
  18.2 64.2 all-gather.3
  85.4 61.3 all-gather.5
  153.9 10.3 reduce-scatter.2
  196.3 11.9 reduce-scatter.4

commit v2 on v0

v2 whole, which is shorter than its diff:
```python
import functools
import math

import jax
import jax.numpy as jnp
from jax import lax
from jax.experimental import pallas as pl
from jax.experimental.pallas import tpu as pltpu
from jax.sharding import PartitionSpec as P

DH = 128
EPS = 1e-5
THETA = 500000.0
FC = 512
NS = 8
COLORS = (
    (0, 24, (2, 1, 0)),
    (24, 24, (1, 0, 2)),
    (48, 16, (0, 2, 1)),
)


def layer_kernel(
    x_ref, cs_ref, g1_ref, g2_ref, wq_ref, wk_ref, wv_ref, wo_ref, w1_ref, w3_ref, w2_ref,
    out_ref,
    xa, csa, act, wkv, w1s, w3s, w2s, kv, qb, fm, ob, mb, lb, ot, part, got, gotz, h1, hid,
    wsem, wkvsem, xs, xr, cps, cpr, as_, ar, bs, br, cs_, cr, fs, fr, ys, yr, zs, zr,
):
    j = lax.axis_index('tp')
    c = lax.axis_index('cp')
    co = (c // 16, (c // 4) % 4, c % 4)
    stride = (16, 4, 1)
    dm = x_ref.shape[1]
    nf = w1_ref.shape[1]
    nch = -(-nf // FC)
    pp = x_ref.shape[0] // 2

    def peer(d, t):
        return c + ((co[d] + t) % 4 - co[d]) * stride[d]

    def width(i):
        return min(FC, nf - i * FC)

    def cp_w1(i):
        n = width(i)
        return (pltpu.make_async_copy(w1_ref.at[:, pl.ds(i * FC, n)], w1s.at[i % NS, :, pl.ds(0, n)], wsem.at[0, i % NS]),
                pltpu.make_async_copy(w3_ref.at[:, pl.ds(i * FC, n)], w3s.at[i % NS, :, pl.ds(0, n)], wsem.at[1, i % NS]))

    def cp_w2(i):
        n = width(i)
        s = i % (NS + 1)
        return (pltpu.make_async_copy(w2_ref.at[pl.ds(i * FC, n), :], w2s.at[s, pl.ds(0, n), :], wsem.at[2, s]),)

    def cp_kv():
        return (pltpu.make_async_copy(wk_ref, wkv.at[:, pl.ds(0, DH)], wkvsem.at[0]),
                pltpu.make_async_copy(wv_ref, wkv.at[:, pl.ds(DH, DH)], wkvsem.at[1]))

    def cp_q():
        return (pltpu.make_async_copy(wq_ref.at[:, pl.ds(0, FC)], w1s.at[NS - 1], wsem.at[0, NS - 1]),
                pltpu.make_async_copy(wq_ref.at[:, pl.ds(FC, FC)], w3s.at[NS - 1], wsem.at[1, NS - 1]))

    def cp_o():
        return (pltpu.make_async_copy(wo_ref.at[pl.ds(0, FC), :], w2s.at[NS - 1], wsem.at[2, NS - 1]),
                pltpu.make_async_copy(wo_ref.at[pl.ds(FC, FC), :], w2s.at[NS], wsem.at[2, NS]))

    def start(cps_):
        for q in cps_:
            q.start()

    def wait(cps_):
        for q in cps_:
            q.wait()

    start(cp_kv())
    start(cp_q())

    bar = pltpu.get_barrier_semaphore()
    pl.semaphore_signal(bar, inc=1, device_id={'tp': 1 - j})
    for d in range(3):
        for t in (1, 2, 3):
            pl.semaphore_signal(bar, inc=1, device_id={'cp': peer(d, t)})

    lo = pl.multiple_of(j * pp, pp)
    hi = pl.multiple_of((3 - j) * pp, pp)
    own = (lo, hi)

    for i in range(2):
        xa[pl.ds(own[i], pp), :] = x_ref[pl.ds(i * pp, pp), :]
        csa[pl.ds(own[i], pp), :] = cs_ref[pl.ds(i * pp, pp), :]

    r = lax.broadcasted_iota(jnp.int32, fm.shape[1:], 0)
    qi = lax.broadcasted_iota(jnp.int32, fm.shape[1:], 1) % 32
    rr = r % 32
    cc = ((r // 128 + co[1]) % 4) * 4 + (r // 32 + co[2]) % 4
    fm[0] = cc * 32 + rr - qi
    fm[1] = rr - cc * 32 - qi

    pl.semaphore_wait(bar, 10)

    def cp_x():
        out = []
        for i in range(2):
            out.append(pltpu.make_async_remote_copy(
                x_ref.at[pl.ds(i * pp, pp), :], xa.at[pl.ds(own[i], pp), :], xs.at[i], xr.at[i], device_id={'tp': 1 - j}))
            out.append(pltpu.make_async_remote_copy(
                cs_ref.at[pl.ds(i * pp, pp), :], csa.at[pl.ds(own[i], pp), :], cps.at[i], cpr.at[i], device_id={'tp': 1 - j}))
        return out

    start(cp_x())

    start(cp_o())
    for i in range(min(NS - 1, nch)):
        start(cp_w1(i))
        start(cp_w2(i))

    def norm(v, g):
        vf = v.astype(jnp.float32)
        inv = lax.rsqrt(jnp.mean(vf * vf, axis=-1, keepdims=True) + EPS)
        return (vf * inv * g.astype(jnp.float32)).astype(jnp.bfloat16)

    for q in cp_x():
        q.wait_recv()
    act[...] = norm(xa[...], g1_ref[...])

    ca = csa[:, 0:DH]
    sa = csa[:, DH:2 * DH]

    def rope(u):
        return (u * ca + pltpu.roll(u, DH // 2, 1) * sa).astype(jnp.bfloat16)

    wait(cp_kv())
    kvf = jnp.dot(act[...], wkv[...], preferred_element_type=jnp.float32)
    kv[0, 0, 0, 0] = rope(kvf[:, 0:DH])
    kv[1, 0, 0, 0] = kvf[:, DH:2 * DH].astype(jnp.bfloat16)

    def region(col, sel, half=slice(None)):
        r0, n, order = COLORS[col]
        idx = [0, 0, 0]
        for d, s in zip(order, sel):
            idx[d] = s
        return kv.at[(half, idx[0], idx[1], idx[2], pl.ds(r0, n), slice(None))]

    def cp_a(col, k, t):
        d = COLORS[col][2][k]
        dst = [0, 0, 0]
        dst[k] = (4 - t) % 4
        return pltpu.make_async_remote_copy(
            region(col, (0, 0, 0)), region(col, dst), as_.at[col, k, t - 1], ar.at[col, k, t - 1],
            device_id={'cp': peer(d, t)})

    def cp_b(col, k, t):
        d = COLORS[col][2][k]
        dst = [pl.ds(1, 3), 0, 0]
        dst[k] = (4 - t) % 4
        return pltpu.make_async_remote_copy(
            region(col, (pl.ds(1, 3), 0, 0)), region(col, dst), bs.at[col, k - 1, t - 1], br.at[col, k - 1, t - 1],
            device_id={'cp': peer(d, t)})

    def cp_c(col, t):
        d = COLORS[col][2][2]
        return pltpu.make_async_remote_copy(
            region(col, (pl.ds(0, 4), pl.ds(1, 3), 0)), region(col, (pl.ds(0, 4), pl.ds(1, 3), (4 - t) % 4)),
            cs_.at[col, t // 2], cr.at[col, t // 2], device_id={'cp': peer(d, t)})

    def cp_f(col, t):
        d = COLORS[col][2][2]
        return pltpu.make_async_remote_copy(
            region(col, (pl.ds(0, 4), pl.ds(1, 3), (4 - t) % 4), t // 2),
            region(col, (pl.ds(0, 4), pl.ds(1, 3), 2), t // 2),
            fs.at[col, t // 2], fr.at[col, t // 2], device_id={'cp': peer(d, t)})

    for k in range(3):
        for col in range(3):
            for t in (1, 3, 2):
                cp_a(col, k, t).start()

    wait(cp_q())
    for half, wref in ((0, w1s), (1, w3s)):
        qf = jnp.dot(act[...], wref[NS - 1], preferred_element_type=jnp.float32)
        for h in range(4):
            qh = rope(qf[:, h * DH:(h + 1) * DH])
            hh = half * 4 + h
            qb[0, pl.ds(hh * 32, 32), :] = qh[0:32]
            qb[1, pl.ds(hh * 32, 32), :] = qh[32:64]
    if nch > NS - 1:
        start(cp_w1(NS - 1))

    for col in range(3):
        for t in (1, 3, 2):
            cp_a(col, 0, t).wait_recv()
        for k in (1, 2):
            for t in (1, 3, 2):
                cp_b(col, k, t).start()
    for col in range(3):
        for t in (1, 3, 2):
            cp_a(col, 1, t).wait_recv()
            cp_b(col, 1, t).wait_recv()
        for t in (1, 3):
            cp_c(col, t).start()
    for col in range(3):
        for t in (1, 3):
            cp_c(col, t).wait_recv()
            cp_f(col, t).start()
    for col in range(3):
        for t in (1, 3, 2):
            cp_a(col, 2, t).wait_recv()
            cp_b(col, 2, t).wait_recv()
        for t in (1, 3):
            cp_f(col, t).wait_recv()

    mb[...] = jnp.full_like(mb, -1e30)
    lb[...] = jnp.zeros_like(lb)
    ot[...] = jnp.zeros_like(ot)
    scale = math.log2(math.e) / math.sqrt(DH)
    z = co[0]
    ownp = co[1] * 4 + co[2]

    def unit(u, carry):
        v = u - 4
        first = u < 4
        low = v <= z
        half = jnp.where(first, 1, jnp.where(low, 0, 1))
        reg = jnp.where(first, 0, jnp.where(low, 0, 1))
        blk = jnp.where(first, u, jnp.where(low, v, v - 1))
        lim = jnp.where(first, 1 << 20, jnp.where(low, ownp * 32 + (z - v) * 512, (v - 1 - z) * 512 - ownp * 32))
        dz = (blk - z + 4) % 4
        rows = pl.ds(pl.multiple_of(reg * 32, 32), 32)
        kb = kv[0, dz, :, :, rows, :].reshape(512, DH)
        vb = kv[1, dz, :, :, rows, :].reshape(512, DH)
        s = lax.dot_general(kb, qb[half], (((1,), (1,)), ((), ())), preferred_element_type=jnp.float32) * scale
        s = jnp.where(fm[reg] <= lim, s, -1e30)
        m0 = mb[half]
        m1 = jnp.maximum(m0, jnp.max(s, axis=0, keepdims=True))
        al = jnp.exp2(m0 - m1)
        e = jnp.exp2(s - m1)
        lb[half] = lb[half] * al + jnp.sum(e, axis=0, keepdims=True)
        pv = lax.dot_general(vb, e.astype(jnp.bfloat16), (((0,), (0,)), ((), ())), preferred_element_type=jnp.float32)
        ot[half] = ot[half] * al + pv
        mb[half] = m1
        return carry

    lax.fori_loop(0, 9, unit, 0)

    for half in range(2):
        o = (ot[half] / lb[half]).T.astype(jnp.bfloat16)
        for h in range(8):
            ob[pl.ds(half * 32, 32), pl.ds(h * DH, DH)] = o[h * 32:(h + 1) * 32]

    wait(cp_o())
    part[...] = (jnp.dot(ob[:, 0:FC], w2s[NS - 1], preferred_element_type=jnp.float32)
                 + jnp.dot(ob[:, FC:2 * FC], w2s[NS], preferred_element_type=jnp.float32))
    cp_y = pltpu.make_async_remote_copy(part, got, ys, yr, device_id={'tp': 1 - j})
    cp_y.start()
    for i in (NS - 1, NS):
        if i < nch:
            start(cp_w2(i))
    cp_y.wait()
    h1[...] = (xa[...].astype(jnp.float32) + (part[...] + got[...])).astype(jnp.bfloat16)
    act[...] = norm(h1[...], g2_ref[...])

    def up(i):
        n = width(i)
        wait(cp_w1(i))
        u = jnp.dot(act[...], w1s[i % NS, :, 0:n], preferred_element_type=jnp.float32)
        g = jnp.dot(act[...], w3s[i % NS, :, 0:n], preferred_element_type=jnp.float32)
        hid[i % 2, :, 0:n] = (u * jax.nn.sigmoid(u) * g).astype(jnp.bfloat16)
        if i + NS < nch:
            start(cp_w1(i + NS))

    def down(i):
        n = width(i)
        wait(cp_w2(i))
        zz = jnp.dot(hid[i % 2, :, 0:n], w2s[i % (NS + 1), 0:n, :], preferred_element_type=jnp.float32)
        if i == 0:
            part[...] = zz
        else:
            part[...] += zz
        if i + NS + 1 < nch:
            start(cp_w2(i + NS + 1))

    for i in range(nch + 1):
        if i < nch:
            up(i)
        if i > 0:
            down(i - 1)

    oth = (pl.multiple_of((1 - j) * pp, pp), pl.multiple_of((2 + j) * pp, pp))
    cp_z = [pltpu.make_async_remote_copy(part.at[pl.ds(oth[i], pp), :], gotz.at[pl.ds(i * pp, pp), :], zs.at[i], zr.at[i],
                                         device_id={'tp': 1 - j}) for i in range(2)]
    start(cp_z)
    for i in range(2):
        cp_z[i].wait_recv()
        sl = pl.ds(own[i], pp)
        out_ref[pl.ds(i * pp, pp), :] = (
            h1[sl, :].astype(jnp.float32) + (part[sl, :] + gotz[pl.ds(i * pp, pp), :])).astype(jnp.bfloat16)

    for q in cp_z:
        q.wait_send()
    for q in cp_x():
        q.wait_send()
    for col in range(3):
        for t in (1, 2, 3):
            for k in range(3):
                cp_a(col, k, t).wait_send()
            for k in (1, 2):
                cp_b(col, k, t).wait_send()
        for t in (1, 3):
            cp_c(col, t).wait_send()
            cp_f(col, t).wait_send()


def solution(mesh):
    tok = P(('dp', 'cp', 'tp'), None)
    col = P(None, 'tp')
    row = P('tp', None)

    def local(x, pos, g1, g2, wq, wk, wv, wo, w1, w3, w2):
        rows, dm = x.shape
        freq = 1.0 / (THETA ** (jnp.arange(0, DH, 2, dtype=jnp.float32) / DH))
        ang = pos.astype(jnp.float32)[:, None] * freq
        cos, sin = jnp.cos(ang), jnp.sin(ang)
        cs = jnp.concatenate([cos, cos, -sin, sin], axis=-1)
        bf, f32 = jnp.bfloat16, jnp.float32
        sem = pltpu.SemaphoreType.DMA
        vm = pltpu.VMEM
        vs = pl.BlockSpec(memory_space=pltpu.VMEM)
        anys = pl.BlockSpec(memory_space=pl.ANY)
        scratch = [
            vm((2 * rows, dm), bf),
            vm((2 * rows, 2 * DH), f32),
            vm((2 * rows, dm), bf),
            vm((dm, 2 * DH), bf),
            vm((NS, dm, FC), bf),
            vm((NS, dm, FC), bf),
            vm((NS + 1, FC, dm), bf),
            vm((2, 4, 4, 4, 2 * rows, DH), bf),
            vm((2, 256, DH), bf),
            vm((2, 512, 256), jnp.int32),
            vm((2 * rows, 8 * DH), bf),
            vm((2, 1, 256), f32),
            vm((2, 1, 256), f32),
            vm((2, DH, 256), f32),
            vm((2 * rows, dm), f32),
            vm((2 * rows, dm), f32),
            vm((rows, dm), f32),
            vm((2 * rows, dm), bf),
            vm((2, 2 * rows, FC), bf),
            sem((3, NS + 1)), sem((2,)),
            sem((2,)), sem((2,)), sem((2,)), sem((2,)),
            sem((3, 3, 3)), sem((3, 3, 3)),
            sem((3, 2, 3)), sem((3, 2, 3)),
            sem((3, 2)), sem((3, 2)),
            sem((3, 2)), sem((3, 2)),
            sem, sem, sem((2,)), sem((2,)),
        ]
        return pl.pallas_call(
            layer_kernel,
            name='layer',
            out_shape=jax.ShapeDtypeStruct((rows, dm), bf),
            in_specs=[vs] * 4 + [anys] * 7,
            out_specs=vs,
            scratch_shapes=scratch,
            compiler_params=pltpu.CompilerParams(
                collective_id=0, has_side_effects=True, vmem_limit_bytes=67043328),
        )(x, cs, g1.reshape(1, dm), g2.reshape(1, dm), wq, wk, wv, wo, w1, w3, w2)

    return jax.shard_map(local, mesh=mesh, in_specs=(tok, P(('dp', 'cp', 'tp')), P(None), P(None), col, col, col, row, col, col, row), out_specs=tok, check_vma=False)
```

time: 447 us -> 59 us (0.13)
  blocking collectives: 302 us -> 0 us
  waiting for transfers between devices: 71.6 us -> 0 us
  Pallas kernels: 0 us -> 53.1 us
  matrix products: 43.2 us -> 0 us
  between operations: 14.6 us -> 0.01 us
  other arithmetic: 8.25 us -> 1.51 us
    unnamed x2 -> x0, blocking collectives: 298 us -> none
    reduce_scatter x2 -> x0, waiting for transfers between devices: 71.5 us -> none  [the longest x1 59.4 us: local(): lax.psum_scatter(jnp.dot(o, wo, preferred_element_type=jnp.float32), 'tp'...]
    pallas_call x0 -> x1, Pallas kernels: none -> 53.1 us  [local(): pl.pallas_call(layer_kernel, name='layer', out_shape=jax.ShapeDtypeStruct...]
    dot_general x8 -> x0, matrix products: 43.2 us -> none  [the longest x1 18.9 us: local(): jnp.dot(hid, w2, preferred_element_type=jnp.float32)]
    unnamed x21 -> x1, local copies, waits for them, and re-layouts: 6.34 us -> 1.57 us
  transfers between devices with their start and end apart: 4 -> 0, of which waited for: 2 -> 0; matrix products, arithmetic and copies ran while one was open for 2% -> 0% of each run, Pallas kernels for 0% -> 0%
where the time goes in v2:
time: 59 us; the launch traced here: 58.8 us
  Pallas kernels  53.1 us (90%)
  local copies, waits for them, and re-layouts  4.15 us (7%)
  other arithmetic  1.51 us (3%)
    pallas_call x1, Pallas kernels, local(): pl.pallas_call(layer_kernel, name='layer', out_shape=jax.ShapeDtypeStruct...  53.1 us
    unnamed x1, local copies, waits for them, and re-layouts  1.57 us
    reshape x1, local copies, waits for them, and re-layouts, local(): g1.reshape(1, dm)  1.29 us
    reshape x1, local copies, waits for them, and re-layouts, local(): g2.reshape(1, dm)  1.29 us

profile of v2, /device:TPU:1, one launch (start us, length us, event | category | flops | bytes accessed | tf_op | source)
XLA Modules:
  0.0 58.8 jit_solution(2249928501664677063)
XLA Ops:
  0.0 0.7 %convert_element_type.3 = f32[32]{0:T(128)S(1)} convert(s32[32]{0:T(128)} %param.12) | non-fusion elementwise | flops 32 | bytes 256 | tf_op jit(solution)/shard_map/convert_element_type | solution.py:320
  0.7 1.3 %reshape.13.g1_ref = bf16[1,2048]{1,0:T(2,128)(2,1)} reshape(bf16[2048]{0:T(1024)(128)(2,1)} %param.13) | data formatting | bytes 8192 | tf_op jit(solution)/shard_map/reshape | solution.py:365
  2.0 1.3 %reshape.14.g2_ref = bf16[1,2048]{1,0:T(2,128)(2,1)} reshape(bf16[2048]{0:T(1024)(128)(2,1)} %param.14) | data formatting | bytes 8192 | tf_op jit(solution)/shard_map/reshape | solution.py:365
  3.2 0.1 multiply_cosine_fusion
  3.4 0.7 %pad_maximum_fusion.cs_ref = f32[32,256]{1,0:T(8,128)} fusion(f32[32,64]{1,0:T(8,128)S(1)} %get-tuple-element.7, f32[32,64]{1,0:T(8,128)S(1)} %get-tuple-element.6, f32[32,64]{1,0:T(8,128)S(1)} %get-tuple-element.5), kind=kLoop, calls=%fused_computation | loop fusion | flops 24576 | bytes 57344 | tf_op jit(solution)/shard_map/concatenate | solution.py:322
  4.1 53.1 %layer.1 = bf16[32,2048]{1,0:T(8,128)(2,1)} custom-call(bf16[32,2048]{1,0:T(8,128)(2,1)} %x_ref.1, f32[32,256]{1,0:T(8,128)} %pad_maximum_fusion.cs_ref, bf16[1,2048]{1,0:T(2,128)(2,1)} %reshape.13.g1_ref, bf16[1,2048]{1,0:T(2,128)(2,1)} %reshape.14.g2_ref, bf16[2048,1024]{1,0:T(8,128)(2,1)} %wq_ref.1, bf16[2048,128]{1,0:T(8,128)(2,1)} %wk_ref.1, ...), custom_call_target="tpu_custom_call" | custom-call | tf_op jit(solution)/shard_map/layer/pallas_call | solution.py:356
  57.2 1.6 %copy.13 = bf16[32,2048]{1,0:T(8,128)(2,1)} copy(bf16[32,2048]{1,0:T(8,128)(2,1)} %layer.1) | data formatting | bytes 262144
  (1 shorter events, 0.0 us)
